TPU v7x, 32 devices: a whole 2x2x4 slice. The times are simulated.
32 devices in a mesh: seq: 32 (over z, y, x, core).
Axes of the slice: x: 2, y: 2, z: 4, core: 2. Of those that a mesh axis runs over, the one named last changes fastest.
Arguments:
- queries: bfloat16 [4096, 4096], P('seq'), may hold values from -48 to 48, as said below
- keys: bfloat16 [4096, 512], P('seq'), may hold values from -6 to 6, as said below
- values: bfloat16 [4096, 512], P('seq'), may hold values from -6 to 6
Outputs:
- attended: bfloat16 [4096, 4096], P('seq')
Inputs may be any that keep to these rules, and one draw needn't show every extreme that they name: queries of every block, with 32 heads of 128 entries per token. keys of every block, with 4 heads of 128 entries per token.
All inputs are finite; a program needn't handle non-finite values.
Results may differ from a plain program's by a relative error of at most 0.0049.
Values may be sent and summed in bfloat16 or wider, within the bound.
A program may use at most 64 MiB of HBM per device.

v0:
```python
import functools
import math

import jax
import jax.numpy as jnp
from jax import lax
from jax.experimental import pallas as pl
from jax.experimental.pallas import tpu as pltpu
from jax.sharding import PartitionSpec as P

KEY_VALUE_HEADS = 4
HEAD_SIZE = 128
HALO = 64
SUM_ROWS = 8
MESH = pl.DeviceIdType.MESH

BLOCK = 32
CHILDREN = {
    0: (9, 3, 5, 1),
    3: (19, 6, 2),
    5: (7, 13, 4),
    7: (14,),
    9: (21, 17, 11),
    11: (15, 10),
    13: (8, 12),
    17: (25, 16),
    19: (23, 27, 18),
    21: (31, 29, 20),
    23: (22,),
    25: (24,),
    27: (26,),
    29: (28,),
    31: (30,),
}
RELAYS = {3: 1, 5: 2, 7: 3, 9: 2, 11: 3, 13: 3, 17: 3, 19: 3, 21: 3, 23: 4, 25: 4, 27: 3, 29: 4, 31: 4}


def plan(n):
    if n % BLOCK == 0:
        return BLOCK, CHILDREN, RELAYS
    chain = {d: (d + 1,) for d in range(n - 1)}
    return n, chain, {d: 4 for d in range(1, n - 1)}


def pick(here, table):
    value = 0
    for place, entry in table.items():
        value = jnp.where(here == place, entry, value)
    return value


def packed(fields, base):
    return sum(field * base**i for i, field in enumerate(fields))


def kernel(
    n,
    q_hbm,
    k_hbm,
    v_hbm,
    out,
    q,
    loc,
    halo,
    anc,
    acc,
    total,
    top,
    q_sem,
    loc_sem,
    halo_sem,
    send_sem,
    recv_sem,
):
    me = lax.axis_index("seq")
    tokens = q_hbm.shape[0]
    heads = q_hbm.shape[1] // HEAD_SIZE
    group = heads // KEY_VALUE_HEADS
    factor = math.log2(math.e) / math.sqrt(HEAD_SIZE)
    every = tuple(range(KEY_VALUE_HEADS))

    for h in every:
        columns = pl.ds(h * HEAD_SIZE, HEAD_SIZE)
        for side, ref in enumerate((k_hbm, v_hbm)):
            pltpu.make_async_copy(ref.at[:, columns], loc.at[h, side], loc_sem).start()
    query_copy = pltpu.make_async_copy(q_hbm, q, q_sem)
    query_copy.start()

    block, tree, relays = plan(n)
    here = me % block
    origin = me - here
    base = block + 1
    above = {d: set() for d in range(block)}
    for d, below in tree.items():
        for child in below:
            above[child].add(d)
    for d in range(1, block):
        above[d].add(d - 1)
    ready_table = {
        d: sum(d in others for others in above.values()) for d in range(block)
    }

    barrier = pltpu.get_barrier_semaphore()
    most = max(len(others) for others in above.values())
    parents = pick(
        here, {d: packed([p + 1 for p in sorted(o)], base) for d, o in above.items()}
    )
    for i in range(most):
        parent = (parents // base**i) % base

        @pl.when(parent > 0)
        def _(parent=parent):
            pl.semaphore_signal(
                barrier,
                inc=1,
                device_id=(origin + parent - 1,),
                device_id_type=MESH,
            )

    ready = pick(here, ready_table)
    if n > block:
        @pl.when((here == 0) & (me > 0))
        def _():
            for target in (me - block, me - 1):
                pl.semaphore_signal(
                    barrier, inc=1, device_id=(target,), device_id_type=MESH
                )

        across = jnp.where((here == 0) | (here == block - 1), 1, 0)
        ready = ready + jnp.where(me + block < n, across, 0)
        ready = ready + jnp.where(
            (here == block - 1) & (me + block >= n) & (me < n - 1), 1, 0
        )

    slots = max(len(below) for below in tree.values())
    code = pick(
        here, {d: packed([c + 1 for c in below], base) for d, below in tree.items()}
    )
    children = []
    for i in range(slots):
        child = (code // base**i) % base
        children.append((child > 0, origin + child - 1))
    turn = pick(here, relays)
    if n > block:
        turn = jnp.where((here == 0) & (me > 0), 1, turn)
        children.append(((here == 0) & (me + block < n), me + block))

    def to_child(source, target, slot, arrival):
        return pltpu.make_async_remote_copy(
            src_ref=source,
            dst_ref=target,
            send_sem=send_sem.at[slot],
            recv_sem=arrival,
            device_id=(children[slot][1],),
            device_id_type=MESH,
        )

    def forward(source, h, side):
        for slot, (condition, _) in enumerate(children):

            @pl.when(condition)
            def _(slot=slot):
                to_child(
                    source.at[h, side], anc.at[h, side], slot, recv_sem.at[h, side]
                ).start()

    @pl.when(ready > 0)
    def _():
        pl.semaphore_wait(barrier, ready)

    pltpu.make_async_copy(loc, loc, loc_sem).wait()

    halo_copy = pltpu.make_async_remote_copy(
        src_ref=loc.at[:, :, pl.ds(tokens - HALO, HALO)],
        dst_ref=halo,
        send_sem=halo_sem.at[0],
        recv_sem=halo_sem.at[1],
        device_id=((me + 1) % n,),
        device_id_type=MESH,
    )

    @pl.when(me == 0)
    def _():
        for h in every:
            for side in range(2):
                forward(loc, h, side)

    @pl.when(me < n - 1)
    def _():
        halo_copy.start()

    def take(h, side):
        pltpu.make_async_remote_copy(
            src_ref=anc.at[h, side],
            dst_ref=anc.at[h, side],
            send_sem=send_sem.at[0],
            recv_sem=recv_sem.at[h, side],
            device_id=((me + 1) % n,),
            device_id_type=MESH,
        ).wait_recv()

    def pass_on(h):
        for side in range(2):
            take(h, side)
            forward(anc, h, side)

    def relay(which):
        @pl.when(turn == which)
        def _():
            for h in every:
                pass_on(h)

    rows = group * tokens

    def stacked(h):
        first = h * group
        return jnp.concatenate(
            [
                q[:, (first + i) * HEAD_SIZE : (first + i + 1) * HEAD_SIZE]
                for i in range(group)
            ],
            axis=0,
        )

    def scores(h, key):
        return lax.dot_general(
            key, stacked(h), (((1,), (1,)), ((), ())), preferred_element_type=jnp.float32
        )

    def flipped(value):
        ones = jnp.ones((2 * SUM_ROWS, value.shape[0]), value.dtype)
        return jnp.concatenate([value.T, ones], axis=0)

    def mix(weights, value):
        both = jnp.dot(
            flipped(value),
            weights.astype(jnp.bfloat16),
            preferred_element_type=jnp.float32,
        )
        return both[:HEAD_SIZE], both[HEAD_SIZE : HEAD_SIZE + SUM_ROWS]

    def put(h, mixed, summed):
        first = h * group
        result = (mixed * (1.0 / summed[:1])).astype(out.dtype)
        for i in range(group):
            out[:, (first + i) * HEAD_SIZE : (first + i + 1) * HEAD_SIZE] = result[
                :, i * tokens : (i + 1) * tokens
            ].T

    relay(1)

    key_ids = lax.broadcasted_iota(jnp.int32, (tokens, rows), 0)
    query_ids = lax.broadcasted_iota(jnp.int32, (tokens, rows), 1) % tokens
    visible = key_ids <= query_ids
    query_copy.wait()
    for h in every:
        s = jnp.where(visible, scores(h, loc[h, 0]), -1e30)
        highest = jnp.max(s, axis=0, keepdims=True)
        mixed, summed = mix(jnp.exp2((s - highest) * factor), loc[h, 1])
        acc[h] = mixed
        total[h] = summed
        top[h] = jnp.broadcast_to(highest, (SUM_ROWS, rows))

    @pl.when(me == 0)
    def _():
        for h in every:
            put(h, acc[h], total[h])

    relay(2)

    def merged(h, key, value):
        s = scores(h, key)
        before = top[h]
        highest = jnp.maximum(before, jnp.max(s, axis=0, keepdims=True))
        drop = jnp.exp2((before - highest) * factor)
        mixed, summed = mix(jnp.exp2((s - highest[:1]) * factor), value)
        mixed = mixed + acc[h] * drop[:1]
        summed = summed + total[h] * drop
        return mixed, summed, highest

    @pl.when(me > 0)
    def _():
        halo_copy.wait_recv()
        for h in every:
            mixed, summed, highest = merged(h, halo[h, 0], halo[h, 1])
            acc[h] = mixed
            total[h] = summed
            top[h] = highest
        relay(3)
        for h in every:

            @pl.when(turn == 0)
            def _(h=h):
                for side in range(2):
                    take(h, side)

            @pl.when(turn == 4)
            def _(h=h):
                pass_on(h)

            mixed, summed, _ = merged(h, anc[h, 0], anc[h, 1])
            put(h, mixed, summed)

    @pl.when((turn > 0) | (me == 0))
    def _():
        for slot, (condition, _) in enumerate(children):

            @pl.when(condition)
            def _(slot=slot):
                to_child(anc, anc, slot, recv_sem.at[0, 0]).wait_send()

    @pl.when(me < n - 1)
    def _():
        halo_copy.wait_send()


def attention(n, queries, keys, values):
    tokens, width = queries.shape
    rows = width // HEAD_SIZE // KEY_VALUE_HEADS * tokens
    block, tree, _ = plan(n)
    slots = max(len(below) for below in tree.values()) + (n > block)
    state = pltpu.VMEM((KEY_VALUE_HEADS, HEAD_SIZE, rows), jnp.float32)
    row = pltpu.VMEM((KEY_VALUE_HEADS, SUM_ROWS, rows), jnp.float32)
    pieces = (KEY_VALUE_HEADS, 2, tokens, HEAD_SIZE)
    return pl.pallas_call(
        functools.partial(kernel, n),
        out_shape=pltpu.VMEM(queries.shape, queries.dtype),
        in_specs=[pl.BlockSpec(memory_space=pltpu.HBM)] * 3,
        out_specs=pl.BlockSpec(memory_space=pltpu.VMEM),
        scratch_shapes=[
            pltpu.VMEM(queries.shape, queries.dtype),
            pltpu.VMEM(pieces, keys.dtype),
            pltpu.VMEM((KEY_VALUE_HEADS, 2, HALO, HEAD_SIZE), keys.dtype),
            pltpu.VMEM(pieces, keys.dtype),
            state,
            row,
            row,
            pltpu.SemaphoreType.DMA,
            pltpu.SemaphoreType.DMA,
            pltpu.SemaphoreType.DMA((2,)),
            pltpu.SemaphoreType.DMA((slots,)),
            pltpu.SemaphoreType.DMA((KEY_VALUE_HEADS, 2)),
        ],
        compiler_params=pltpu.CompilerParams(
            collective_id=0, has_side_effects=True, vmem_limit_bytes=60 * 2**20
        ),
    )(queries, keys, values)


def solution(mesh):
    n = mesh.shape["seq"]
    return jax.shard_map(
        functools.partial(attention, n),
        mesh=mesh,
        in_specs=(P("seq", None), P("seq", None), P("seq", None)),
        out_specs=P("seq", None),
        check_vma=False,
    )
```

profile of v0, /device:TPU:28, one launch (start us, length us, event | category | flops | bytes accessed | tf_op | source)
XLA Modules:
  0.0 14.5 jit_solution(1965697227415628247)
XLA Ops:
  0.0 13.5 %shard_map.37 = bf16[128,4096]{1,0:T(8,128)(2,1)S(1)} custom-call(bf16[128,4096]{1,0:T(8,128)(2,1)} %q_hbm.1, bf16[128,512]{1,0:T(8,128)(2,1)} %k_hbm.1, bf16[128,512]{1,0:T(8,128)(2,1)} %v_hbm.1), custom_call_target="tpu_custom_call" | custom-call | tf_op jit(solution)/shard_map/pallas_call | solution.py:325
  13.5 1.0 %copy.5 = bf16[128,4096]{1,0:T(8,128)(2,1)} copy(bf16[128,4096]{1,0:T(8,128)(2,1)S(1)} %shard_map.37) | data formatting | bytes 2097152
where the time goes:
time: 14.6 us; the launch traced here: 14.5 us
  Pallas kernels  13.5 us (92%)
  local copies, waits for them, and re-layouts  0.97 us (7%)
    pallas_call x1, Pallas kernels, attention(): pl.pallas_call(functools.partial(kernel, n), out_shape=pltpu.VMEM(queries...  13.5 us
    unnamed x1, local copies, waits for them, and re-layouts  0.97 us

commit v1 on v0

--- a/solution.py
+++ b/solution.py
@@ -15,31 +15,53 @@
 MESH = pl.DeviceIdType.MESH
 
 BLOCK = 32
-CHILDREN = {
-    0: (9, 3, 5, 1),
-    3: (19, 6, 2),
-    5: (7, 13, 4),
-    7: (14,),
-    9: (21, 17, 11),
-    11: (15, 10),
-    13: (8, 12),
-    17: (25, 16),
-    19: (23, 27, 18),
-    21: (31, 29, 20),
+KEY_CHILDREN = {
+    0: (3, 5, 9, 1,),
+    1: (15,),
+    3: (27, 7, 2,),
+    5: (13, 4,),
+    7: (23, 6,),
+    9: (17, 11, 8,),
+    11: (10,),
+    13: (29, 12,),
+    15: (14,),
+    17: (19, 21, 25, 16,),
+    19: (18,),
+    21: (20,),
     23: (22,),
     25: (24,),
-    27: (26,),
+    27: (31, 26,),
     29: (28,),
     31: (30,),
 }
-RELAYS = {3: 1, 5: 2, 7: 3, 9: 2, 11: 3, 13: 3, 17: 3, 19: 3, 21: 3, 23: 4, 25: 4, 27: 3, 29: 4, 31: 4}
+VALUE_CHILDREN = {
+    0: (3, 9, 5, 1,),
+    3: (27, 7, 2,),
+    5: (4,),
+    7: (23, 6,),
+    9: (13, 17, 11, 8,),
+    11: (10,),
+    13: (29, 15, 12,),
+    15: (14,),
+    17: (19, 21, 25, 16,),
+    19: (18,),
+    21: (20,),
+    23: (22,),
+    25: (24,),
+    27: (31, 26,),
+    29: (28,),
+    31: (30,),
+}
+TURN = {1: 2, 3: 1, 5: 2, 7: 3, 9: 1, 11: 4, 13: 3, 15: 4, 17: 3, 19: 4, 21: 4, 23: 4, 25: 4, 27: 2, 29: 4, 31: 4}
+LATE_HALO = {1: 1, 2: 1, 4: 1, 21: 1, 27: 1}
+HALO_LAST = (2, 4, 8, 26, )
 
 
 def plan(n):
     if n % BLOCK == 0:
-        return BLOCK, CHILDREN, RELAYS
+        return BLOCK, (KEY_CHILDREN, VALUE_CHILDREN), TURN, LATE_HALO, HALO_LAST
     chain = {d: (d + 1,) for d in range(n - 1)}
-    return n, chain, {d: 4 for d in range(1, n - 1)}
+    return n, (chain, chain), {d: 4 for d in range(1, n - 1)}, {}, ()
 
 
 def pick(here, table):
@@ -86,14 +108,15 @@
     query_copy = pltpu.make_async_copy(q_hbm, q, q_sem)
     query_copy.start()
 
-    block, tree, relays = plan(n)
+    block, trees, turns, late_halo, halo_last = plan(n)
     here = me % block
     origin = me - here
     base = block + 1
     above = {d: set() for d in range(block)}
-    for d, below in tree.items():
-        for child in below:
-            above[child].add(d)
+    for tree in trees:
+        for d, below in tree.items():
+            for child in below:
+                above[child].add(d)
     for d in range(1, block):
         above[d].add(d - 1)
     ready_table = {
@@ -132,36 +155,42 @@
             (here == block - 1) & (me + block >= n) & (me < n - 1), 1, 0
         )
 
-    slots = max(len(below) for below in tree.values())
-    code = pick(
-        here, {d: packed([c + 1 for c in below], base) for d, below in tree.items()}
-    )
+    slots = max(len(below) for tree in trees for below in tree.values())
     children = []
-    for i in range(slots):
-        child = (code // base**i) % base
-        children.append((child > 0, origin + child - 1))
-    turn = pick(here, relays)
+    for tree in trees:
+        code = pick(
+            here, {d: packed([c + 1 for c in below], base) for d, below in tree.items()}
+        )
+        targets = []
+        for i in range(slots):
+            child = (code // base**i) % base
+            targets.append((child > 0, origin + child - 1))
+        if n > block:
+            targets.append(((here == 0) & (me + block < n), me + block))
+        children.append(targets)
+    turn = pick(here, turns)
+    late = pick(here, late_halo)
+    last = pick(here, {d: 1 for d in halo_last})
     if n > block:
         turn = jnp.where((here == 0) & (me > 0), 1, turn)
-        children.append(((here == 0) & (me + block < n), me + block))
-
-    def to_child(source, target, slot, arrival):
+
+    def to_child(source, target, slot, side, arrival):
         return pltpu.make_async_remote_copy(
             src_ref=source,
             dst_ref=target,
-            send_sem=send_sem.at[slot],
+            send_sem=send_sem.at[slot, side],
             recv_sem=arrival,
-            device_id=(children[slot][1],),
+            device_id=(children[side][slot][1],),
             device_id_type=MESH,
         )
 
     def forward(source, h, side):
-        for slot, (condition, _) in enumerate(children):
+        for slot, (condition, _) in enumerate(children[side]):
 
             @pl.when(condition)
             def _(slot=slot):
                 to_child(
-                    source.at[h, side], anc.at[h, side], slot, recv_sem.at[h, side]
+                    source.at[h, side], anc.at[h, side], slot, side, recv_sem.at[h, side]
                 ).start()
 
     @pl.when(ready > 0)
@@ -185,9 +214,12 @@
             for side in range(2):
                 forward(loc, h, side)
 
-    @pl.when(me < n - 1)
-    def _():
-        halo_copy.start()
+    def send_halo(which):
+        @pl.when((me < n - 1) & (late == which))
+        def _():
+            halo_copy.start()
+
+    send_halo(0)
 
     def take(h, side):
         pltpu.make_async_remote_copy(
@@ -248,6 +280,7 @@
             ].T
 
     relay(1)
+    send_halo(3)
 
     key_ids = lax.broadcasted_iota(jnp.int32, (tokens, rows), 0)
     query_ids = lax.broadcasted_iota(jnp.int32, (tokens, rows), 1) % tokens
@@ -266,7 +299,9 @@
         for h in every:
             put(h, acc[h], total[h])
 
+    send_halo(1)
     relay(2)
+    send_halo(2)
 
     def merged(h, key, value):
         s = scores(h, key)
@@ -278,36 +313,53 @@
         summed = summed + total[h] * drop
         return mixed, summed, highest
 
-    @pl.when(me > 0)
+    def keep(h, mixed, summed, highest):
+        acc[h] = mixed
+        total[h] = summed
+        top[h] = highest
+
+    def take_head(h):
+        @pl.when(turn == 0)
+        def _():
+            for side in range(2):
+                take(h, side)
+
+        @pl.when(turn == 4)
+        def _():
+            pass_on(h)
+
+    @pl.when((me > 0) & (last == 0))
     def _():
         halo_copy.wait_recv()
         for h in every:
-            mixed, summed, highest = merged(h, halo[h, 0], halo[h, 1])
-            acc[h] = mixed
-            total[h] = summed
-            top[h] = highest
+            keep(h, *merged(h, halo[h, 0], halo[h, 1]))
         relay(3)
         for h in every:
-
-            @pl.when(turn == 0)
-            def _(h=h):
-                for side in range(2):
-                    take(h, side)
-
-            @pl.when(turn == 4)
-            def _(h=h):
-                pass_on(h)
-
+            take_head(h)
             mixed, summed, _ = merged(h, anc[h, 0], anc[h, 1])
             put(h, mixed, summed)
 
+    if halo_last:
+
+        @pl.when((me > 0) & (last == 1))
+        def _():
+            for h in every:
+                take_head(h)
+                keep(h, *merged(h, anc[h, 0], anc[h, 1]))
+            halo_copy.wait_recv()
+            for h in every:
+                mixed, summed, _ = merged(h, halo[h, 0], halo[h, 1])
+                put(h, mixed, summed)
+
     @pl.when((turn > 0) | (me == 0))
     def _():
-        for slot, (condition, _) in enumerate(children):
-
-            @pl.when(condition)
-            def _(slot=slot):
-                to_child(anc, anc, slot, recv_sem.at[0, 0]).wait_send()
+        for side in range(2):
+            for slot, (condition, _) in enumerate(children[side]):
+
+                @pl.when(condition)
+                def _(slot=slot, side=side):
+                    half = anc.at[:, side]
+                    to_child(half, half, slot, side, recv_sem.at[0, 0]).wait_send()
 
     @pl.when(me < n - 1)
     def _():
@@ -317,8 +369,8 @@
 def attention(n, queries, keys, values):
     tokens, width = queries.shape
     rows = width // HEAD_SIZE // KEY_VALUE_HEADS * tokens
-    block, tree, _ = plan(n)
-    slots = max(len(below) for below in tree.values()) + (n > block)
+    block, trees, *_ = plan(n)
+    slots = max(len(below) for tree in trees for below in tree.values()) + (n > block)
     state = pltpu.VMEM((KEY_VALUE_HEADS, HEAD_SIZE, rows), jnp.float32)
     row = pltpu.VMEM((KEY_VALUE_HEADS, SUM_ROWS, rows), jnp.float32)
     pieces = (KEY_VALUE_HEADS, 2, tokens, HEAD_SIZE)
@@ -338,7 +390,7 @@
             pltpu.SemaphoreType.DMA,
             pltpu.SemaphoreType.DMA,
             pltpu.SemaphoreType.DMA((2,)),
-            pltpu.SemaphoreType.DMA((slots,)),
+            pltpu.SemaphoreType.DMA((slots, 2)),
             pltpu.SemaphoreType.DMA((KEY_VALUE_HEADS, 2)),
         ],
         compiler_params=pltpu.CompilerParams(

time: 14.6 us -> 12.5 us (0.86)
  the two profiles are of different devices: /device:TPU:28 before, /device:TPU:9 now
where the time goes in v1:
time: 12.5 us; the launch traced here: 12.4 us
  Pallas kernels  11.4 us (91%)
  local copies, waits for them, and re-layouts  0.97 us (8%)
    pallas_call x1, Pallas kernels, attention(): pl.pallas_call(functools.partial(kernel, n), out_shape=pltpu.VMEM(queries...  11.4 us
    unnamed x1, local copies, waits for them, and re-layouts  0.97 us

profile of v1, /device:TPU:9, one launch (start us, length us, event | category | flops | bytes accessed | tf_op | source)
XLA Modules:
  0.0 12.4 jit_solution(14295781185117852069)
XLA Ops:
  0.0 11.4 %shard_map.37 = bf16[128,4096]{1,0:T(8,128)(2,1)S(1)} custom-call(bf16[128,4096]{1,0:T(8,128)(2,1)} %q_hbm.1, bf16[128,512]{1,0:T(8,128)(2,1)} %k_hbm.1, bf16[128,512]{1,0:T(8,128)(2,1)} %v_hbm.1), custom_call_target="tpu_custom_call" | custom-call | tf_op jit(solution)/shard_map/pallas_call | solution.py:377
  11.4 1.0 %copy.5 = bf16[128,4096]{1,0:T(8,128)(2,1)} copy(bf16[128,4096]{1,0:T(8,128)(2,1)S(1)} %shard_map.37) | data formatting | bytes 2097152

commit v2 on v1

v2 whole, which is shorter than its diff:
```python
import functools
import math

import jax
import jax.numpy as jnp
from jax import lax
from jax.experimental import pallas as pl
from jax.experimental.pallas import tpu as pltpu
from jax.sharding import PartitionSpec as P

KEY_VALUE_HEADS = 4
HEAD_SIZE = 128
HALO = 64
SUM_ROWS = 8
MESH = pl.DeviceIdType.MESH

BLOCK = 32
KEY_CHILDREN = {
    0: (9, 5, 3, 1,),
    3: (27, 7, 2,),
    5: (29, 4,),
    7: (23, 6,),
    9: (13, 8, 11, 17,),
    11: (10,),
    13: (12, 15,),
    15: (14,),
    17: (21, 19, 25, 16,),
    19: (18,),
    21: (20,),
    23: (22,),
    25: (24,),
    27: (26, 31,),
    29: (28,),
    31: (30,),
}
VALUE_CHILDREN = {
    0: (5, 3, 9, 1,),
    1: (14,),
    3: (27, 7, 2,),
    5: (29, 4,),
    7: (23, 6,),
    9: (11, 13, 17, 8,),
    11: (10,),
    13: (15, 12,),
    17: (21, 19, 25, 16,),
    19: (18,),
    21: (20,),
    23: (22,),
    25: (24,),
    27: (26, 31,),
    29: (28,),
    31: (30,),
}
TURN = {0: 5, 1: 4, 2: 1, 3: 0, 4: 4, 5: 1, 6: 3, 7: 4, 8: 4, 9: 0, 10: 3, 11: 4, 12: 3, 13: 2, 14: 3, 15: 3, 16: 4, 17: 0, 18: 4, 19: 4, 20: 3, 21: 3, 22: 4, 23: 4, 24: 4, 25: 4, 26: 4, 27: 1, 28: 4, 29: 4, 30: 3, 31: 3}
LATE_HALO = {1: 1, 4: 1, 8: 1, 15: 1, 16: 1, 20: 1, 24: 1, 25: 1, 26: 1, 27: 1, 29: 1}


def plan(n):
    if n % BLOCK == 0:
        return BLOCK, (KEY_CHILDREN, VALUE_CHILDREN), TURN, LATE_HALO
    chain = {d: (d + 1,) for d in range(n - 1)}
    return n, (chain, chain), {d: 3 if d else 5 for d in range(n)}, {}


def pick(here, table):
    value = 0
    for place, entry in table.items():
        value = jnp.where(here == place, entry, value)
    return value


def packed(fields, base):
    return sum(field * base**i for i, field in enumerate(fields))


def kernel(
    n,
    q_hbm,
    k_hbm,
    v_hbm,
    out,
    q,
    flat,
    kv,
    acc,
    total,
    top,
    q_sem,
    loc_sem,
    halo_sem,
    send_sem,
    recv_sem,
):
    me = lax.axis_index("seq")
    tokens = q_hbm.shape[0]
    heads = q_hbm.shape[1] // HEAD_SIZE
    group = heads // KEY_VALUE_HEADS
    factor = math.log2(math.e) / math.sqrt(HEAD_SIZE)
    every = tuple(range(KEY_VALUE_HEADS))
    rows = group * tokens

    before = tokens + HALO
    anchor = pl.ds(0, tokens)
    halo = pl.ds(tokens, HALO)
    own = pl.ds(before, tokens)

    for h in every:
        columns = pl.ds(h * HEAD_SIZE, HEAD_SIZE)
        for side, ref in enumerate((k_hbm, v_hbm)):
            pltpu.make_async_copy(
                ref.at[:, columns], kv.at[h, side, own], loc_sem
            ).start()
    query_copy = pltpu.make_async_copy(q_hbm, q, q_sem)
    query_copy.start()

    block, trees, turns, late_halo = plan(n)
    here = me % block
    origin = me - here
    base = block + 1
    above = {d: set() for d in range(block)}
    for tree in trees:
        for d, below in tree.items():
            for child in below:
                above[child].add(d)
    for d in range(1, block):
        above[d].add(d - 1)
    ready_table = {
        d: sum(d in others for others in above.values()) for d in range(block)
    }

    barrier = pltpu.get_barrier_semaphore()
    most = max(len(others) for others in above.values())
    parents = pick(
        here, {d: packed([p + 1 for p in sorted(o)], base) for d, o in above.items()}
    )
    for i in range(most):
        parent = (parents // base**i) % base

        @pl.when(parent > 0)
        def _(parent=parent):
            pl.semaphore_signal(
                barrier,
                inc=1,
                device_id=(origin + parent - 1,),
                device_id_type=MESH,
            )

    ready = pick(here, ready_table)
    if n > block:
        @pl.when((here == 0) & (me > 0))
        def _():
            for target in (me - block, me - 1):
                pl.semaphore_signal(
                    barrier, inc=1, device_id=(target,), device_id_type=MESH
                )

        across = jnp.where((here == 0) | (here == block - 1), 1, 0)
        ready = ready + jnp.where(me + block < n, across, 0)
        ready = ready + jnp.where(
            (here == block - 1) & (me + block >= n) & (me < n - 1), 1, 0
        )

    slots = max(len(below) for tree in trees for below in tree.values())
    children = []
    for tree in trees:
        code = pick(
            here, {d: packed([c + 1 for c in below], base) for d, below in tree.items()}
        )
        targets = []
        for i in range(slots):
            child = (code // base**i) % base
            targets.append((child > 0, origin + child - 1))
        if n > block:
            targets.append(((here == 0) & (me + block < n), me + block))
        children.append(targets)
    turn = pick(here, turns)
    late = pick(here, late_halo)
    if n > block:
        turn = jnp.where((here == 0) & (me > 0), 0, turn)

    def to_child(rows_sent, h, slot, side):
        return pltpu.make_async_remote_copy(
            src_ref=kv.at[h, side, rows_sent],
            dst_ref=kv.at[h, side, anchor],
            send_sem=send_sem.at[slot, side],
            recv_sem=recv_sem.at[h, side],
            device_id=(children[side][slot][1],),
            device_id_type=MESH,
        )

    def forward(rows_sent, h, side):
        for slot, (condition, _) in enumerate(children[side]):

            @pl.when(condition)
            def _(slot=slot):
                to_child(rows_sent, h, slot, side).start()

    query_copy.wait()
    for i in range(heads):
        flat[:, i * tokens : (i + 1) * tokens] = q[
            :, i * HEAD_SIZE : (i + 1) * HEAD_SIZE
        ].T

    @pl.when(ready > 0)
    def _():
        pl.semaphore_wait(barrier, ready)

    pltpu.make_async_copy(kv.at[:, :, own], kv.at[:, :, own], loc_sem).wait()

    halo_copy = pltpu.make_async_remote_copy(
        src_ref=kv.at[:, :, pl.ds(before + tokens - HALO, HALO)],
        dst_ref=kv.at[:, :, halo],
        send_sem=halo_sem.at[0],
        recv_sem=halo_sem.at[1],
        device_id=((me + 1) % n,),
        device_id_type=MESH,
    )

    def send_halo(which):
        @pl.when((me < n - 1) & (late == which))
        def _():
            halo_copy.start()

    send_halo(0)

    @pl.when(me == 0)
    def _():
        for h in every:
            for side in range(2):
                forward(own, h, side)

    def pass_on(h):
        for side in range(2):
            pltpu.make_async_remote_copy(
                src_ref=kv.at[h, side, anchor],
                dst_ref=kv.at[h, side, anchor],
                send_sem=send_sem.at[0, side],
                recv_sem=recv_sem.at[h, side],
                device_id=((me + 1) % n,),
                device_id_type=MESH,
            ).wait_recv()
            forward(anchor, h, side)

    def pass_all():
        for h in every:
            pass_on(h)

    def scores(h, first, stop):
        return jnp.dot(
            kv[h, 0, first:stop],
            flat[:, h * rows : (h + 1) * rows],
            preferred_element_type=jnp.float32,
        )

    def weigh(s, highest):
        return jnp.exp2((s - highest) * factor).astype(jnp.bfloat16)

    def mix(h, first, stop, weights):
        value = kv[h, 1, first:stop]
        ones = jnp.ones((2 * SUM_ROWS, stop - first), value.dtype)
        both = jnp.dot(
            jnp.concatenate([value.T, ones], axis=0),
            weights,
            preferred_element_type=jnp.float32,
        )
        return both[:HEAD_SIZE], both[HEAD_SIZE : HEAD_SIZE + SUM_ROWS]

    def put(h, mixed, summed):
        first = h * group
        result = (mixed * (1.0 / summed[:1])).astype(out.dtype)
        for i in range(group):
            out[:, (first + i) * HEAD_SIZE : (first + i + 1) * HEAD_SIZE] = result[
                :, i * tokens : (i + 1) * tokens
            ].T

    def keep(h, mixed, summed, highest):
        acc[h] = mixed
        total[h] = summed
        top[h] = jnp.broadcast_to(highest, (SUM_ROWS, rows))

    def merged(h, first, stop):
        s = scores(h, first, stop)
        was = top[h]
        highest = jnp.maximum(was, jnp.max(s, axis=0, keepdims=True))
        drop = jnp.exp2((was - highest) * factor)
        mixed, summed = mix(h, first, stop, weigh(s, highest[:1]))
        mixed = mixed + acc[h] * drop[:1]
        summed = summed + total[h] * drop
        return mixed, summed, highest

    key_ids = lax.broadcasted_iota(jnp.int32, (tokens, rows), 0)
    query_ids = lax.broadcasted_iota(jnp.int32, (tokens, rows), 1) % tokens
    visible = key_ids <= query_ids

    @pl.when(turn == 0)
    def _():
        pass_all()
        send_halo(3)
        halo_copy.wait_recv()
        for h in every:
            s = scores(h, 0, before + tokens)
            others, mine = s[:before], jnp.where(visible, s[before:], -1e30)
            highest = jnp.maximum(
                jnp.max(others, axis=0, keepdims=True),
                jnp.max(mine, axis=0, keepdims=True),
            )
            weights = jnp.concatenate(
                [weigh(others, highest), weigh(mine, highest)], axis=0
            )
            put(h, *mix(h, 0, before + tokens, weights))

    @pl.when(turn > 0)
    def _():
        for h in every:
            s = jnp.where(visible, scores(h, before, before + tokens), -1e30)
            highest = jnp.max(s, axis=0, keepdims=True)
            mixed, summed = mix(h, before, before + tokens, weigh(s, highest))
            keep(h, mixed, summed, highest)

    @pl.when(me == 0)
    def _():
        for h in every:
            put(h, acc[h], total[h])

    send_halo(1)

    @pl.when(turn == 1)
    def _():
        pass_all()
        send_halo(2)

    @pl.when((turn == 1) | (turn == 4))
    def _():
        halo_copy.wait_recv()
        for h in every:

            @pl.when(turn == 4)
            def _(h=h):
                pass_on(h)

            mixed, summed, _ = merged(h, 0, before)
            put(h, mixed, summed)

    @pl.when((turn == 2) | (turn == 3))
    def _():
        halo_copy.wait_recv()
        for h in every:
            keep(h, *merged(h, tokens, before))

        @pl.when(turn == 2)
        def _():
            pass_all()

        for h in every:

            @pl.when(turn == 3)
            def _(h=h):
                pass_on(h)

            mixed, summed, _ = merged(h, 0, tokens)
            put(h, mixed, summed)

    for side in range(2):
        for slot, (condition, _) in enumerate(children[side]):

            @pl.when(condition)
            def _(slot=slot, side=side):
                sent = kv.at[:, side, anchor]
                pltpu.make_async_remote_copy(
                    src_ref=sent,
                    dst_ref=sent,
                    send_sem=send_sem.at[slot, side],
                    recv_sem=recv_sem.at[0, side],
                    device_id=(children[side][slot][1],),
                    device_id_type=MESH,
                ).wait_send()

    @pl.when(me < n - 1)
    def _():
        halo_copy.wait_send()


def attention(n, queries, keys, values):
    tokens, width = queries.shape
    rows = width // HEAD_SIZE // KEY_VALUE_HEADS * tokens
    block, trees, *_ = plan(n)
    slots = max(len(below) for tree in trees for below in tree.values()) + (n > block)
    state = pltpu.VMEM((KEY_VALUE_HEADS, HEAD_SIZE, rows), jnp.float32)
    row = pltpu.VMEM((KEY_VALUE_HEADS, SUM_ROWS, rows), jnp.float32)
    pieces = (KEY_VALUE_HEADS, 2, 2 * tokens + HALO, HEAD_SIZE)
    return pl.pallas_call(
        functools.partial(kernel, n),
        out_shape=pltpu.VMEM(queries.shape, queries.dtype),
        in_specs=[pl.BlockSpec(memory_space=pltpu.HBM)] * 3,
        out_specs=pl.BlockSpec(memory_space=pltpu.VMEM),
        scratch_shapes=[
            pltpu.VMEM(queries.shape, queries.dtype),
            pltpu.VMEM((HEAD_SIZE, KEY_VALUE_HEADS * rows), queries.dtype),
            pltpu.VMEM(pieces, keys.dtype),
            state,
            row,
            row,
            pltpu.SemaphoreType.DMA,
            pltpu.SemaphoreType.DMA,
            pltpu.SemaphoreType.DMA((2,)),
            pltpu.SemaphoreType.DMA((slots, 2)),
            pltpu.SemaphoreType.DMA((KEY_VALUE_HEADS, 2)),
        ],
        compiler_params=pltpu.CompilerParams(
            collective_id=0, has_side_effects=True, vmem_limit_bytes=60 * 2**20
        ),
    )(queries, keys, values)


def solution(mesh):
    n = mesh.shape["seq"]
    return jax.shard_map(
        functools.partial(attention, n),
        mesh=mesh,
        in_specs=(P("seq", None), P("seq", None), P("seq", None)),
        out_specs=P("seq", None),
        check_vma=False,
    )
```

time: 12.5 us -> 12.1 us (0.968)
  the two profiles are of different devices: /device:TPU:9 before, /device:TPU:14 now
where the time goes in v2:
time: 12.1 us; the launch traced here: 11.9 us
  Pallas kernels  10.9 us (90%)
  local copies, waits for them, and re-layouts  0.97 us (8%)
    pallas_call x1, Pallas kernels, attention(): pl.pallas_call(functools.partial(kernel, n), out_shape=pltpu.VMEM(queries...  10.9 us
    unnamed x1, local copies, waits for them, and re-layouts  0.97 us

profile of v2, /device:TPU:14, one launch (start us, length us, event | category | flops | bytes accessed | tf_op | source)
XLA Modules:
  0.0 11.9 jit_solution(8798492016221835260)
XLA Ops:
  0.0 10.9 %shard_map.37 = bf16[128,4096]{1,0:T(8,128)(2,1)S(1)} custom-call(bf16[128,4096]{1,0:T(8,128)(2,1)} %q_hbm.1, bf16[128,512]{1,0:T(8,128)(2,1)} %k_hbm.1, bf16[128,512]{1,0:T(8,128)(2,1)} %v_hbm.1), custom_call_target="tpu_custom_call" | custom-call | tf_op jit(solution)/shard_map/pallas_call | solution.py:391
  10.9 1.0 %copy.5 = bf16[128,4096]{1,0:T(8,128)(2,1)} copy(bf16[128,4096]{1,0:T(8,128)(2,1)S(1)} %shard_map.37) | data formatting | bytes 2097152

commit v3 on v2

--- a/solution.py
+++ b/solution.py
@@ -12,6 +12,7 @@
 HEAD_SIZE = 128
 HALO = 64
 SUM_ROWS = 8
+PARTS = 2
 MESH = pl.DeviceIdType.MESH
 
 BLOCK = 32
@@ -20,9 +21,9 @@
     3: (27, 7, 2,),
     5: (29, 4,),
     7: (23, 6,),
-    9: (13, 8, 11, 17,),
-    11: (10,),
-    13: (12, 15,),
+    9: (11, 8, 13, 17,),
+    11: (10, 15,),
+    13: (12,),
     15: (14,),
     17: (21, 19, 25, 16,),
     19: (18,),
@@ -35,13 +36,13 @@
 }
 VALUE_CHILDREN = {
     0: (5, 3, 9, 1,),
-    1: (14,),
     3: (27, 7, 2,),
     5: (29, 4,),
     7: (23, 6,),
-    9: (11, 13, 17, 8,),
-    11: (10,),
-    13: (15, 12,),
+    9: (11, 17, 13, 8,),
+    11: (15, 10,),
+    13: (12,),
+    15: (14,),
     17: (21, 19, 25, 16,),
     19: (18,),
     21: (20,),
@@ -51,8 +52,8 @@
     29: (28,),
     31: (30,),
 }
-TURN = {0: 5, 1: 4, 2: 1, 3: 0, 4: 4, 5: 1, 6: 3, 7: 4, 8: 4, 9: 0, 10: 3, 11: 4, 12: 3, 13: 2, 14: 3, 15: 3, 16: 4, 17: 0, 18: 4, 19: 4, 20: 3, 21: 3, 22: 4, 23: 4, 24: 4, 25: 4, 26: 4, 27: 1, 28: 4, 29: 4, 30: 3, 31: 3}
-LATE_HALO = {1: 1, 4: 1, 8: 1, 15: 1, 16: 1, 20: 1, 24: 1, 25: 1, 26: 1, 27: 1, 29: 1}
+TURN = {0: 5, 1: 3, 2: 1, 3: 0, 4: 4, 5: 1, 6: 3, 7: 4, 8: 4, 9: 0, 10: 3, 11: 2, 12: 3, 13: 3, 14: 3, 15: 3, 16: 4, 17: 0, 18: 4, 19: 4, 20: 3, 21: 3, 22: 4, 23: 4, 24: 4, 25: 4, 26: 4, 27: 1, 28: 4, 29: 4, 30: 3, 31: 3}
+LATE_HALO = {1: 4, 4: 1, 8: 1, 15: 1, 16: 1, 20: 1, 24: 1, 25: 1, 26: 1, 27: 1, 29: 1}
 
 
 def plan(n):
@@ -178,22 +179,24 @@
     if n > block:
         turn = jnp.where((here == 0) & (me > 0), 0, turn)
 
-    def to_child(rows_sent, h, slot, side):
+    size = tokens // PARTS
+
+    def to_child(start, h, slot, side, part):
         return pltpu.make_async_remote_copy(
-            src_ref=kv.at[h, side, rows_sent],
-            dst_ref=kv.at[h, side, anchor],
+            src_ref=kv.at[h, side, pl.ds(start + part * size, size)],
+            dst_ref=kv.at[h, side, pl.ds(part * size, size)],
             send_sem=send_sem.at[slot, side],
-            recv_sem=recv_sem.at[h, side],
+            recv_sem=recv_sem.at[h, side, part],
             device_id=(children[side][slot][1],),
             device_id_type=MESH,
         )
 
-    def forward(rows_sent, h, side):
+    def forward(start, h, side, part):
         for slot, (condition, _) in enumerate(children[side]):
 
             @pl.when(condition)
             def _(slot=slot):
-                to_child(rows_sent, h, slot, side).start()
+                to_child(start, h, slot, side, part).start()
 
     query_copy.wait()
     for i in range(heads):
@@ -227,19 +230,22 @@
     def _():
         for h in every:
             for side in range(2):
-                forward(own, h, side)
+                for part in range(PARTS):
+                    forward(before, h, side, part)
 
     def pass_on(h):
         for side in range(2):
-            pltpu.make_async_remote_copy(
-                src_ref=kv.at[h, side, anchor],
-                dst_ref=kv.at[h, side, anchor],
-                send_sem=send_sem.at[0, side],
-                recv_sem=recv_sem.at[h, side],
-                device_id=((me + 1) % n,),
-                device_id_type=MESH,
-            ).wait_recv()
-            forward(anchor, h, side)
+            for part in range(PARTS):
+                piece = kv.at[h, side, pl.ds(part * size, size)]
+                pltpu.make_async_remote_copy(
+                    src_ref=piece,
+                    dst_ref=piece,
+                    send_sem=send_sem.at[0, side],
+                    recv_sem=recv_sem.at[h, side, part],
+                    device_id=((me + 1) % n,),
+                    device_id_type=MESH,
+                ).wait_recv()
+                forward(0, h, side, part)
 
     def pass_all():
         for h in every:
@@ -346,6 +352,7 @@
         halo_copy.wait_recv()
         for h in every:
             keep(h, *merged(h, tokens, before))
+        send_halo(4)
 
         @pl.when(turn == 2)
         def _():
@@ -370,7 +377,7 @@
                     src_ref=sent,
                     dst_ref=sent,
                     send_sem=send_sem.at[slot, side],
-                    recv_sem=recv_sem.at[0, side],
+                    recv_sem=recv_sem.at[0, side, 0],
                     device_id=(children[side][slot][1],),
                     device_id_type=MESH,
                 ).wait_send()
@@ -404,7 +411,7 @@
             pltpu.SemaphoreType.DMA,
             pltpu.SemaphoreType.DMA((2,)),
             pltpu.SemaphoreType.DMA((slots, 2)),
-            pltpu.SemaphoreType.DMA((KEY_VALUE_HEADS, 2)),
+            pltpu.SemaphoreType.DMA((KEY_VALUE_HEADS, 2, PARTS)),
         ],
         compiler_params=pltpu.CompilerParams(
             collective_id=0, has_side_effects=True, vmem_limit_bytes=60 * 2**20

time: 12.1 us -> 11.8 us (0.975)
  the two profiles are of different devices: /device:TPU:14 before, /device:TPU:22 now
where the time goes in v3:
time: 11.8 us; the launch traced here: 11.7 us
  Pallas kernels  10.7 us (91%)
  local copies, waits for them, and re-layouts  0.97 us (8%)
    pallas_call x1, Pallas kernels, attention(): pl.pallas_call(functools.partial(kernel, n), out_shape=pltpu.VMEM(queries...  10.7 us
    unnamed x1, local copies, waits for them, and re-layouts  0.97 us

profile of v3, /device:TPU:22, one launch (start us, length us, event | category | flops | bytes accessed | tf_op | source)
XLA Modules:
  0.0 11.7 jit_solution(2996736217315113070)
XLA Ops:
  0.0 10.7 %shard_map.37 = bf16[128,4096]{1,0:T(8,128)(2,1)S(1)} custom-call(bf16[128,4096]{1,0:T(8,128)(2,1)} %q_hbm.1, bf16[128,512]{1,0:T(8,128)(2,1)} %k_hbm.1, bf16[128,512]{1,0:T(8,128)(2,1)} %v_hbm.1), custom_call_target="tpu_custom_call" | custom-call | tf_op jit(solution)/shard_map/pallas_call | solution.py:398
  10.7 1.0 %copy.5 = bf16[128,4096]{1,0:T(8,128)(2,1)} copy(bf16[128,4096]{1,0:T(8,128)(2,1)S(1)} %shard_map.37) | data formatting | bytes 2097152

commit v4 on v3

--- a/solution.py
+++ b/solution.py
@@ -52,7 +52,7 @@
     29: (28,),
     31: (30,),
 }
-TURN = {0: 5, 1: 3, 2: 1, 3: 0, 4: 4, 5: 1, 6: 3, 7: 4, 8: 4, 9: 0, 10: 3, 11: 2, 12: 3, 13: 3, 14: 3, 15: 3, 16: 4, 17: 0, 18: 4, 19: 4, 20: 3, 21: 3, 22: 4, 23: 4, 24: 4, 25: 4, 26: 4, 27: 1, 28: 4, 29: 4, 30: 3, 31: 3}
+TURN = {0: 5, 1: 3, 2: 1, 3: 0, 4: 4, 5: 1, 6: 3, 7: 4, 8: 4, 9: 0, 10: 3, 11: 2, 12: 3, 13: 3, 14: 3, 15: 3, 16: 4, 17: 0, 18: 3, 19: 3, 20: 3, 21: 3, 22: 3, 23: 3, 24: 3, 25: 3, 26: 4, 27: 1, 28: 4, 29: 4, 30: 3, 31: 3}
 LATE_HALO = {1: 4, 4: 1, 8: 1, 15: 1, 16: 1, 20: 1, 24: 1, 25: 1, 26: 1, 27: 1, 29: 1}
 
 

time: 11.8 us -> 11.8 us (level)
  no operation moved by 1% of the time
where the time goes in v4:
time: 11.8 us; the launch traced here: 11.6 us
  Pallas kernels  10.6 us (90%)
  local copies, waits for them, and re-layouts  0.97 us (8%)
    pallas_call x1, Pallas kernels, attention(): pl.pallas_call(functools.partial(kernel, n), out_shape=pltpu.VMEM(queries...  10.6 us
    unnamed x1, local copies, waits for them, and re-layouts  0.97 us

profile of v4, /device:TPU:22, one launch (start us, length us, event | category | flops | bytes accessed | tf_op | source)
XLA Modules:
  0.0 11.6 jit_solution(12310341006849755105)
XLA Ops:
  0.0 10.6 %shard_map.37 = bf16[128,4096]{1,0:T(8,128)(2,1)S(1)} custom-call(bf16[128,4096]{1,0:T(8,128)(2,1)} %q_hbm.1, bf16[128,512]{1,0:T(8,128)(2,1)} %k_hbm.1, bf16[128,512]{1,0:T(8,128)(2,1)} %v_hbm.1), custom_call_target="tpu_custom_call" | custom-call | tf_op jit(solution)/shard_map/pallas_call | solution.py:398
  10.6 1.0 %copy.5 = bf16[128,4096]{1,0:T(8,128)(2,1)} copy(bf16[128,4096]{1,0:T(8,128)(2,1)S(1)} %shard_map.37) | data formatting | bytes 2097152
